TPU v7x, 32 devices: a whole 2x2x4 slice. The times are simulated.
32 devices in a mesh: dp: 2 (over x), row: 4 (over z), col: 4 (over y, core).
Axes of the slice: x: 2, y: 2, z: 4, core: 2. Of those that a mesh axis runs over, the one named last changes fastest.
Arguments:
- images_in: bfloat16 [24, 577, 1024], P(('dp', 'row'), None, 'col'), may hold values from -6 to 6
- cotangent: bfloat16 [24, 577, 1024], P(('dp', 'row'), None, 'col'), may hold values from -6 to 6
- first_gain: float32 [1024], P('col'), may hold values from 0.1 to 1.9
- first_shift: float32 [1024], P('col'), may hold values from -3 to 3
- second_gain: float32 [1024], P('col'), may hold values from 0.1 to 1.9
- second_shift: float32 [1024], P('col'), may hold values from -3 to 3
- qkv_weight: bfloat16 [1024, 3, 1024], P('row', None, 'col'), may hold values from -0.1875 to 0.1875
- qv_bias: float32 [2, 1024], P(None, 'col'), may hold values from -3 to 3
- out_weight: bfloat16 [1024, 1024], P('row', 'col'), may hold values from -0.75 to 0.75
- out_bias: float32 [1024], P('col'), may hold values from -3 to 3
- fc1_weight: bfloat16 [1024, 4096], P('row', 'col'), may hold values from -0.1875 to 0.1875
- fc1_bias: float32 [4096], P('col'), may hold values from -3 to 3
- fc2_weight: bfloat16 [1024, 4096], P('row', 'col'), may hold values from -0.09375 to 0.09375
- fc2_bias: float32 [1024], P('col'), may hold values from -3 to 3
- qkv_momentum: float32 [1024, 3, 1024], P('row', None, 'col'), may hold values from -48 to 48
- qkv_variance: float32 [1024, 3, 1024], P('row', None, 'col'), may hold values from 0.1 to 4
- out_momentum: float32 [1024, 1024], P('row', 'col'), may hold values from -15 to 15
- out_variance: float32 [1024, 1024], P('row', 'col'), may hold values from 0.01 to 0.8
- fc1_momentum: float32 [1024, 4096], P('row', 'col'), may hold values from -60 to 60
- fc1_variance: float32 [1024, 4096], P('row', 'col'), may hold values from 0.5 to 10
- fc2_momentum: float32 [1024, 4096], P('row', 'col'), may hold values from -120 to 120
- fc2_variance: float32 [1024, 4096], P('row', 'col'), may hold values from 1 to 40
Outputs:
- images_out: bfloat16 [24, 577, 1024], P(('dp', 'row'), None, 'col')
- images_grad: float32 [24, 577, 1024], P(('dp', 'row'), None, 'col')
- qkv_weight_grad: float32 [1024, 3, 1024], P('row', None, 'col')
- out_weight_grad: float32 [1024, 1024], P('row', 'col')
- fc1_weight_grad: float32 [1024, 4096], P('row', 'col')
- fc2_weight_grad: float32 [1024, 4096], P('row', 'col')
- qv_bias_grad: float32 [2, 1024], P(None, 'col')
- out_bias_grad: float32 [1024], P('col')
- fc1_bias_grad: float32 [4096], P('col')
- fc2_bias_grad: float32 [1024], P('col')
- first_gain_grad: float32 [1024], P('col')
- first_shift_grad: float32 [1024], P('col')
- second_gain_grad: float32 [1024], P('col')
- second_shift_grad: float32 [1024], P('col')
- qkv_weight_new: float32 [1024, 3, 1024], P('row', None, 'col')
- out_weight_new: float32 [1024, 1024], P('row', 'col')
- fc1_weight_new: float32 [1024, 4096], P('row', 'col')
- fc2_weight_new: float32 [1024, 4096], P('row', 'col')
- qkv_momentum_new: float32 [1024, 3, 1024], P('row', None, 'col')
- out_momentum_new: float32 [1024, 1024], P('row', 'col')
- fc1_momentum_new: float32 [1024, 4096], P('row', 'col')
- fc2_momentum_new: float32 [1024, 4096], P('row', 'col')
- qkv_variance_new: float32 [1024, 3, 1024], P('row', None, 'col')
- out_variance_new: float32 [1024, 1024], P('row', 'col')
- fc1_variance_new: float32 [1024, 4096], P('row', 'col')
- fc2_variance_new: float32 [1024, 4096], P('row', 'col')
All inputs are finite; a program needn't handle non-finite values.
Results may differ from a plain program's by a relative error of at most 0.019.
Values may be sent and summed in bfloat16 or wider, within the bound.
A program may use at most 192 MiB of HBM per device.

v0:
```python
import functools

import jax
import jax.numpy as jnp
from jax import lax
from jax.experimental import pallas as pl
from jax.experimental.pallas import tpu as pltpu
from jax.sharding import PartitionSpec as P

HEAD_DIM = 64
STEP = 3


NORM_EPS = 1e-06
LEARN_RATE = 0.02
BETA_FIRST = 0.9
BETA_SECOND = 0.999
ADAM_EPS = 1e-08
WEIGHT_DECAY = 0.05
ROOT_HALF = 0.7071067811865476
ROOT_TWO_PI = 2.5066282746310002
LOG2E = 1.4426950408889634
ROW_TILE = 16
MESH = pl.DeviceIdType.MESH
NT = (((1,), (1,)), ((), ()))
TN = (((0,), (0,)), ((), ()))
F32 = jnp.float32
BF16 = jnp.bfloat16


def copy_to(src, dst, send, recv, where):
    return pltpu.make_async_remote_copy(
        src_ref=src, dst_ref=dst, send_sem=send, recv_sem=recv, device_id=where, device_id_type=MESH
    )


def rel_place(quarter, place):
    return (quarter // 2 + place // 2) % 2 + 2 * ((quarter % 2 + place % 2) % 2)


def crossed(row, code):
    distance = 1
    while distance <= code:
        if code & distance:
            row = row + distance * (1 - 2 * ((row // distance) % 2))
        distance *= 2
    return row


def half_of(dp, full_width):
    half = full_width // 2
    return pl.ds(pl.multiple_of(dp * half, half), half)


def other_half_of(dp, full_width):
    half = full_width // 2
    return pl.ds(pl.multiple_of((1 - dp) * half, half), half)


def row_place(owner, row_count, place, block):
    per = row_count // 4
    at = (rel_place(owner // per, place) * per + owner % per) * block
    return pl.ds(pl.multiple_of(at, block), block)


def part_at(full, rows, cols):
    return full.at[:, rows, cols] if len(full.shape) == 3 else full.at[rows, cols]


def greet(partners):
    barrier = pltpu.get_barrier_semaphore()
    for partner in partners:
        pl.semaphore_signal(barrier, inc=1, device_id=partner, device_id_type=MESH)
    pl.semaphore_wait(barrier, len(partners))


def ahead_kernel(
    sizes,
    images_ref, cot_ref, qkv_ref, out_ref, fc1_ref, fc2_ref,
    gain1_ref, shift1_ref, gain2_ref, shift2_ref, out_bias_ref, qv_bias_ref, fc1_bias_ref, fc2_bias_ref,
    source_out, cot_out, low_out, mixed_out, probs_out, att_out, total_out, grad_out, qkv_out, outw_out, vectors_out,
    move_out, kept_out, fc1_grad_out, fc2_half_out, fc2_grad_out, late_out, bias_out,
    source, cot, low, mixed, probs, att, theirs, given, mine, pair, pair_in, total, qkv_full, out_full, fc1_full, fc2_full, vectors, vectors_ref,
    active, gelu_grad, grad_in, move_given, kept, move, fc1_grad, fc2_grad, dp_in, fc2_half,
    row_send, row_recv, dp_send, dp_recv, own_sem, in_send, in_recv, vec_send, vec_recv, sum_send, sum_recv, image_sem, out_sem,
    back_send, back_recv, half_send, half_recv,
):
    count, seq, rows, local, row_count = sizes
    dp, row, place = lax.axis_index("dp"), lax.axis_index("row"), lax.axis_index("col")
    core_at = {"col": place + 1 - 2 * (place % 2)}
    y_at = {"col": (place + 2) % 4}
    dp_at = {"dp": 1 - dp}
    codes = sorted(range(1, row_count), key=lambda code: -(code & -code))
    fars = [code for code in codes if code & -code == code]
    greet([core_at, y_at, dp_at] + [{"row": crossed(row, far)} for far in fars])
    block = out_ref.shape[0]
    width = 4 * local
    weights = ((qkv_ref, qkv_full), (out_ref, out_full), (fc1_ref, fc1_full), (fc2_ref, fc2_full))

    def row_copy(w, code):
        ref, full = weights[w]
        cols = half_of(dp, full.shape[-1])
        far = code & -code
        held = part_at(full, row_place(crossed(row, code - far), row_count, place, block), cols)
        return copy_to(
            part_at(ref, slice(None), cols) if code == far else held, held, row_send.at[w, code], row_recv.at[w, code], {"row": crossed(row, far)}
        )

    def dp_copy(w, code):
        _, full = weights[w]
        part = part_at(full, row_place(crossed(row, code), row_count, place, block), half_of(dp, full.shape[-1]))
        return copy_to(part, part, dp_send.at[w, code], dp_recv.at[w, code], dp_at)

    def own_copy(w):
        ref, full = weights[w]
        return pltpu.make_async_copy(ref, part_at(full, row_place(row, row_count, place, block), slice(None)), own_sem.at[w])

    inputs = ((images_ref, source), (cot_ref, cot))

    def y_copy(a, i):
        ref, full = inputs[a]
        return copy_to(ref.at[i], full.at[i, :, pl.ds(local, local)], in_send.at[a, 0, i], in_recv.at[a, 0, i], y_at)

    def core_copy(a, i):
        ref, full = inputs[a]
        return copy_to(ref.at[i], full.at[i, :, pl.ds(2 * local, local)], in_send.at[a, 1, i], in_recv.at[a, 1, i], core_at)

    def hand_copy(a, i):
        _, full = inputs[a]
        return copy_to(
            full.at[i, :, pl.ds(local, local)],
            full.at[i, :, pl.ds(3 * local, local)],
            in_send.at[a, 2, i],
            in_recv.at[a, 2, i],
            core_at,
        )

    def here_copy(a, i):
        ref, full = inputs[a]
        return pltpu.make_async_copy(ref.at[i], full.at[i, :, pl.ds(0, local)], in_send.at[a, 3, i])

    def vector_copy(k):
        src = vectors.at[:, pl.ds(local, local)] if k == 2 else vectors_ref
        at = (local, 2 * local, 3 * local)[k]
        return copy_to(
            src, vectors.at[:, pl.ds(at, local)], vec_send.at[k], vec_recv.at[k], (y_at, core_at, core_at)[k]
        )

    for k, vector in enumerate((gain1_ref, shift1_ref, gain2_ref, shift2_ref, out_bias_ref)):
        vectors_ref[k : k + 1, :] = vector[...]
    vectors_ref[5:8, :] = jnp.zeros((3, local), F32)
    vector_here = pltpu.make_async_copy(vectors_ref, vectors.at[:, pl.ds(0, local)], vec_send.at[3])

    def given_copy(i):
        return copy_to(theirs, given.at[i], sum_send.at[0, i], sum_recv.at[0, i], core_at)

    def given_back(i):
        return copy_to(theirs, given.at[i], back_send.at[0, i], back_recv.at[0, i], core_at)

    def pair_back(i):
        return copy_to(pair.at[i], grad_in.at[i], back_send.at[1, i], back_recv.at[1, i], y_at)

    def total_back(i):
        return copy_to(
            total.at[i, :, pl.ds(0, 2 * local)],
            total.at[i, :, pl.ds(2 * local, 2 * local)],
            back_send.at[2, i],
            back_recv.at[2, i],
            core_at,
        )

    def move_copy(i):
        return copy_to(theirs, move_given.at[i], back_send.at[3, i], back_recv.at[3, i], core_at)

    hidden_width = fc1_full.shape[1]

    odd_codes = sorted(range(1, row_count, 2), reverse=True)

    def half_copy(code):
        there = row_place(crossed(row, code), row_count, place, block)
        return copy_to(
            fc2_grad.at[there, other_half_of(dp, hidden_width)], dp_in.at[there, :], half_send.at[code], half_recv.at[code], dp_at
        )

    def pair_copy(i):
        return copy_to(pair.at[i], pair_in.at[i], sum_send.at[1, i], sum_recv.at[1, i], y_at)

    def total_copy(i):
        return copy_to(
            total.at[i, :, pl.ds(0, 2 * local)],
            total.at[i, :, pl.ds(2 * local, 2 * local)],
            sum_send.at[2, i],
            sum_recv.at[2, i],
            core_at,
        )

    def start_own(w):
        for far in fars:
            row_copy(w, far).start()

    def relay(w, code):
        row_copy(w, code).wait_recv()
        for far in fars:
            if far < code & -code:
                row_copy(w, code + far).start()
        dp_copy(w, code).start()

    def arrived(w):
        for code in codes:
            dp_copy(w, code).wait_recv()
        own_copy(w).wait()

    kinds = ((source, source_out), (low, low_out), (mixed, mixed_out), (probs, probs_out), (att, att_out), (total, total_out))

    def image_copy(k, i):
        here, there = kinds[k]
        return pltpu.make_async_copy(here if k in (2, 3) else here.at[i], there.at[i], image_sem.at[k, i])

    wanted = [(a, i) for a in range(2) for i in range(count)]
    start_own(0)
    start_own(1)
    vector_copy(0).start()
    for a, i in wanted:
        y_copy(a, i).start()
    vector_copy(1).start()
    vector_here.start()
    for a, i in wanted:
        core_copy(a, i).start()
        here_copy(a, i).start()
    for w in range(4):
        own_copy(w).start()
    vector_copy(0).wait_recv()
    vector_copy(2).start()
    relay(0, codes[0])
    relay(1, codes[0])
    start_own(2)
    vector_here.wait()
    vector_copy(1).wait_recv()
    vector_copy(2).wait_recv()

    @pl.loop(0, count)
    def _(i):
        y_copy(0, i).wait_recv()
        hand_copy(0, i).start()
        here_copy(0, i).wait()
        core_copy(0, i).wait_recv()
        hand_copy(0, i).wait_recv()
        image_copy(0, i).start()
        values = source[i].astype(F32)
        middle = jnp.sum(values, axis=1, keepdims=True) / width
        square = jnp.sum(values * values, axis=1, keepdims=True) / width
        inverse = lax.rsqrt(square - middle * middle + NORM_EPS)
        low[i] = ((values - middle) * inverse * vectors[0:1, :] + vectors[1:2, :]).astype(BF16)
        image_copy(1, i).start()

        @pl.when(i == 0)
        def _():
            for code in codes[1:]:
                relay(0, code)
                relay(1, code)

    relay(2, codes[0])
    start_own(3)
    arrived(0)
    arrived(1)

    lane = lax.broadcasted_iota(jnp.int32, (1, 2 * HEAD_DIM), 1)
    key_at = lax.broadcasted_iota(jnp.int32, (1, rows), 1)
    pairs = local // (2 * HEAD_DIM)

    @pl.loop(0, count)
    def _(i):
        @pl.when(i > 0)
        def _():
            image_copy(2, i - 1).wait()

        for c in range(3):
            cols = slice(c * local, (c + 1) * local)
            rows_out = jnp.dot(low[i], qkv_full[c], preferred_element_type=F32)
            if c != 1:
                rows_out += qv_bias_ref[c // 2 : c // 2 + 1, :]
            mixed[:, cols] = rows_out.astype(BF16)
        image_copy(2, i).start()

        @pl.when(i > 0)
        def _():
            image_copy(3, i - 1).wait()

        for pair_at in range(pairs):
            base = pair_at * 2 * HEAD_DIM
            queries = mixed[:, base : base + 2 * HEAD_DIM]
            key_rows = mixed[:, local + base : local + base + 2 * HEAD_DIM]
            value_rows = mixed[:, 2 * local + base : 2 * local + base + 2 * HEAD_DIM]
            parts = []
            for side in range(2):
                mask = (lane // HEAD_DIM) == side
                head_q = jnp.where(mask, queries, jnp.zeros_like(queries))
                scores = lax.dot_general(head_q, key_rows, NT, preferred_element_type=F32)
                scores = jnp.where(key_at < seq, scores, -1e30)
                peak = jnp.max(scores, axis=1, keepdims=True)
                powers = jnp.exp2((scores - peak) * (HEAD_DIM**-0.5 * LOG2E))
                share = 1.0 / jnp.sum(powers, axis=1, keepdims=True)
                probs_low = (powers * share).astype(BF16)
                probs[2 * pair_at + side] = probs_low
                parts.append(jnp.dot(probs_low, value_rows, preferred_element_type=F32))
            joined = jnp.where((lane // HEAD_DIM) == 0, parts[0], parts[1])
            att[i, :, 2 * HEAD_DIM * pair_at : 2 * HEAD_DIM * (pair_at + 1)] = joined.astype(BF16)
        image_copy(3, i).start()
        image_copy(4, i).start()
        attended = att[i]

        @pl.when(i > 0)
        def _():
            given_copy(i - 1).wait_send()

        theirs[...] = lax.dot_general(attended, out_full[2 * local :, :], NT, preferred_element_type=F32).astype(BF16)
        given_copy(i).start()
        mine[...] = lax.dot_general(attended, out_full[: 2 * local, :], NT, preferred_element_type=F32)
        given_copy(i).wait_recv()
        pair[i] = (mine[...] + given[i].astype(F32)).astype(BF16)
        pair_copy(i).start()

        @pl.when(i == 0)
        def _():
            for code in codes[1:]:
                relay(2, code)

        @pl.when(i == 1)
        def _():
            for code in codes[:2]:
                relay(3, code)

    for code in codes[2:]:
        relay(3, code)
    outs = ((qkv_full, qkv_out), (out_full, outw_out), (vectors, vectors_out), (cot, cot_out), (move, move_out), (kept, kept_out), (fc1_grad, fc1_grad_out), (fc2_half, fc2_half_out), (fc2_grad, fc2_grad_out), (total.at[pl.ds(0, count - 1)], grad_out))

    def out_copy(k):
        return pltpu.make_async_copy(outs[k][0], outs[k][1], out_sem.at[k])

    for k in range(3):
        out_copy(k).start()
    bias_out[...] = jnp.zeros_like(bias_out)
    step = hidden_width // 4
    given_copy(count - 1).wait_send()
    arrived(2)
    arrived(3)

    @pl.loop(0, count)
    def _(i):
        y_copy(1, i).wait_recv()
        hand_copy(1, i).start()
        pair_copy(i).wait_recv()
        total[i, :, :local] = (pair[i, :, :local].astype(F32) + pair_in[i, :, local:].astype(F32)).astype(BF16)
        total[i, :, local : 2 * local] = (pair[i, :, local:].astype(F32) + pair_in[i, :, :local].astype(F32)).astype(BF16)
        total_copy(i).start()
        image_copy(1, i).wait()
        pair_copy(i).wait_send()
        here_copy(1, i).wait()
        core_copy(1, i).wait_recv()
        hand_copy(1, i).wait_recv()
        bias_out[1:2, :local] += jnp.sum(cot[i, :, :local].astype(F32), axis=0, keepdims=True)
        total_copy(i).wait_recv()
        image_copy(5, i).start()
        values = source[i].astype(F32) + total[i].astype(F32) + vectors[4:5, :]
        kept[i] = values[:, :local] + fc2_bias_ref[...]
        middle = jnp.sum(values, axis=1, keepdims=True) / width
        square = jnp.sum(values * values, axis=1, keepdims=True) / width
        inverse = lax.rsqrt(square - middle * middle + NORM_EPS)
        low[i] = ((values - middle) * inverse * vectors[2:3, :] + vectors[3:4, :]).astype(BF16)
        @pl.loop(0, 4)
        def _(part):
            cols = pl.ds(pl.multiple_of(part * step, step), step)
            pre_act = jnp.dot(low[i], fc1_full[:, cols], preferred_element_type=F32) + fc1_bias_ref[:, cols]
            gate = 0.5 * (1.0 + lax.erf(pre_act * ROOT_HALF))
            active[i, :, cols] = (pre_act * gate).astype(BF16)
            slope = gate + pre_act * jnp.exp(-0.5 * pre_act * pre_act) / ROOT_TWO_PI
            grad_pre = jnp.dot(cot[i], fc2_full[:, cols], preferred_element_type=F32) * slope
            bias_out[0:1, cols] += jnp.sum(grad_pre, axis=0, keepdims=True)
            gelu_grad[i, :, cols] = grad_pre.astype(BF16)

        @pl.when(i > 0)
        def _():
            given_back(i - 1).wait_send()

        theirs[...] = lax.dot_general(gelu_grad[i], fc1_full[2 * local :, :], NT, preferred_element_type=F32).astype(BF16)
        image_copy(5, i).wait()
        given_back(i).start()
        mine[...] = lax.dot_general(gelu_grad[i], fc1_full[: 2 * local, :], NT, preferred_element_type=F32)
        given_back(i).wait_recv()
        pair[i] = (mine[...] + given[i].astype(F32)).astype(BF16)

        @pl.when(i < count - 1)
        def _():
            pair_back(i).start()

    out_copy(3).start()
    late_copy = pltpu.make_async_copy(pair.at[count - 1], late_out, out_sem.at[10])
    late_copy.start()

    def weight_grad(out, left, right):
        @pl.loop(0, 4)
        def _(part):
            span = pl.ds(pl.multiple_of(part * local, local), local)
            terms = [lax.dot_general(left[i, :, span], right[i], TN, preferred_element_type=F32) for i in range(count)]
            out[span, :] = sum(terms[1:], terms[0]).astype(BF16)

    weight_grad(fc2_grad, cot, active)
    for code in odd_codes:
        half_copy(code).start()
    out_copy(8).start()
    given_back(count - 1).wait_send()

    @pl.loop(0, count)
    def _(i):
        @pl.when(i > 0)
        def _():
            move_copy(i - 1).wait_send()

        theirs[...] = lax.dot_general(active[i], fc2_full[2 * local :, :], NT, preferred_element_type=F32).astype(BF16)
        move_copy(i).start()
        mine[...] = lax.dot_general(active[i], fc2_full[: 2 * local, :], NT, preferred_element_type=F32)
        move_copy(i).wait_recv()
        kept[i] += mine[:, :local] + move_given[i, :, :local].astype(F32)
        move[i] = (mine[:, local:] + move_given[i, :, local:].astype(F32)).astype(BF16)

    out_copy(4).start()
    out_copy(5).start()
    weight_grad(fc1_grad, low, gelu_grad)
    out_copy(6).start()

    @pl.loop(0, count - 1)
    def _(i):
        pair_back(i).wait_recv()
        total_copy(i).wait_send()
        total[i, :, :local] = (pair[i, :, :local].astype(F32) + grad_in[i, :, local:].astype(F32)).astype(BF16)
        total[i, :, local : 2 * local] = (pair[i, :, local:].astype(F32) + grad_in[i, :, :local].astype(F32)).astype(BF16)
        total_back(i).start()

        @pl.when(i == count - 2)
        def _():
            for code in odd_codes:
                half_copy(code).wait_recv()
                there = row_place(crossed(row, code), row_count, place, block)
                mine_part = fc2_grad[there, half_of(dp, hidden_width)].astype(F32)
                fc2_half[there, :] = (mine_part + dp_in[there, :].astype(F32)).astype(BF16)
            for code in range(0, row_count, 2):
                there = row_place(crossed(row, code), row_count, place, block)
                fc2_half[there, :] = fc2_grad[there, half_of(dp, hidden_width)]
            out_copy(7).start()

    for i in range(count - 1):
        total_back(i).wait_recv()
    out_copy(9).start()
    for w in range(4):
        for code in codes:
            row_copy(w, code).wait_send()
            dp_copy(w, code).wait_send()
    for a, i in wanted:
        y_copy(a, i).wait_send()
        core_copy(a, i).wait_send()
        hand_copy(a, i).wait_send()
    for k in range(3):
        vector_copy(k).wait_send()
    total_copy(count - 1).wait_send()
    late_copy.wait()
    for i in range(count - 1):
        pair_back(i).wait_send()
        total_back(i).wait_send()
    for i in range(count):
        image_copy(0, i).wait()
        image_copy(4, i).wait()
    move_copy(count - 1).wait_send()
    image_copy(2, count - 1).wait()
    image_copy(3, count - 1).wait()
    for code in odd_codes:
        half_copy(code).wait_send()
    for k in range(len(outs)):
        out_copy(k).wait()


def ahead(images, cotangent, qkv_block, out_block, fc1_block, fc2_block, vectors, qv_bias, fc1_bias, fc2_bias, seq):
    count, rows, local = images.shape
    row_count = lax.axis_size("row")
    width = 4 * local
    heads = local // HEAD_DIM
    hidden = fc1_block.shape[1]

    def wide(*shape):
        return shape, BF16

    all_wide = wide(count, rows, width)
    all_pair = wide(count, rows, 2 * local)
    all_own = wide(count, rows, local)
    own_f32 = ((count, rows, local), F32)
    norm_rows = ((8, width), F32)
    outs = [
        all_wide, all_wide, all_wide, wide(count, rows, 3 * local), wide(count, heads, rows, rows), all_own, all_wide,
        wide(count - 1, rows, width), wide(3, width, local), wide(width, local), norm_rows, all_own, own_f32,
        wide(width, hidden), wide(width, hidden // 2), wide(width, hidden), wide(rows, 2 * local),
        ((2, hidden), F32),
    ]
    scratch = [
        all_wide, all_wide, all_wide, wide(rows, 3 * local), wide(heads, rows, rows), all_own,
        wide(rows, 2 * local), all_pair, ((rows, 2 * local), F32), all_pair, all_pair, all_wide,
        wide(3, width, local), wide(width, local), wide(width, hidden), wide(width, hidden), norm_rows, ((8, local), F32),
        wide(count, rows, hidden), wide(count, rows, hidden), all_pair, all_pair, own_f32, all_own,
        wide(width, hidden), wide(width, hidden), wide(width, hidden // 2), wide(width, hidden // 2),
    ]
    dma = pltpu.SemaphoreType.DMA
    whole = pl.BlockSpec(memory_space=pl.ANY)
    vmem = pl.BlockSpec(memory_space=pltpu.VMEM)
    return pl.pallas_call(
        functools.partial(ahead_kernel, (count, seq, rows, local, row_count)),
        out_shape=[jax.ShapeDtypeStruct(*s) for s in outs],
        in_specs=[whole] * 6 + [vmem] * 8,
        out_specs=[whole] * (len(outs) - 1) + [vmem],
        scratch_shapes=[pltpu.VMEM(*s) for s in scratch]
        + [dma((4, row_count))] * 4
        + [dma((4,)), dma((2, 4, count)), dma((2, 3, count)), dma((4,)), dma((3,))]
        + [dma((3, count)), dma((3, count)), dma((6, count)), dma((11,))]
        + [dma((4, count)), dma((4, count)), dma((row_count,)), dma((row_count,))],
        name="ahead",
        compiler_params=pltpu.CompilerParams(
            vmem_limit_bytes=63 * 2**20, collective_id=0, has_side_effects=True
        ),
    )(images, cotangent, qkv_block, out_block, fc1_block, fc2_block, *vectors, qv_bias, fc1_bias, fc2_bias)


def back_kernel(
    sizes,
    source_ref, total_ref, cot_ref, grad_ref, mixed_ref, probs_ref, att_ref, low_ref, move_ref, kept_ref,
    qkv_ref, outw_ref, fc1_grad_ref, fc2_half_ref, fc2_grad_ref, late_ref, vectors_ref, mlp_bias_ref,
    images_out, images_grad_out, small_out, qkv_out, outw_out, fc1_out, fc2_out,
    source, total, cot, grad_in, mixed, probs, att, low,
    hidden_low, mixed_grad, grad_hidden, normed1, inverse1, qkv_sum, outw_sum, k_turned, v_turned,
    theirs, given, mine, kept_grad, send, got, stat, stat_given, stat_pair, stat_in,
    late_pair, late_in, late_grad, move_in, kept, finished, qkv, outw, qkv_grad, outw_grad, small, small_in,
    half_fc2, half_fc1, half_outw, half_qkv, dp_fc2, dp_fc1, dp_outw, dp_qkv,
    row_fc2, row_fc1, row_outw, row_qkv, tot_fc2, tot_fc1, tot_outw, tot_qkv,
    early_sem, late_sem, once_sem, sum_send, sum_recv, move_send, move_recv, small_send, small_recv,
    dp_send, dp_recv, row_send, row_recv, tot_send, tot_recv, late_send, late_recv, out_sem,
):
    count, rows, local, row_count = sizes
    dp, row, place = lax.axis_index("dp"), lax.axis_index("row"), lax.axis_index("col")
    core_at = {"col": place + 1 - 2 * (place % 2)}
    y_at = {"col": (place + 2) % 4}
    dp_at = {"dp": 1 - dp}
    rounds = [dp_at]
    distance = 1
    while distance < row_count:
        rounds.append({"row": crossed(row, distance)})
        distance *= 2
    greet([core_at, y_at] + rounds)
    width = 4 * local
    block = width // row_count
    two = 2 * HEAD_DIM
    scale = HEAD_DIM**-0.5

    early = ((source_ref, source), (total_ref, total), (cot_ref, cot), (grad_ref, grad_in))
    late = ((mixed_ref, mixed), (probs_ref, probs), (att_ref, att), (low_ref, low))

    def early_load(k, i):
        here, there = early[k]
        return pltpu.make_async_copy(here.at[i], there.at[i % 2] if k == 0 else there, early_sem.at[k])

    def late_load(k, i):
        here, there = late[k]
        return pltpu.make_async_copy(here.at[i], there, late_sem.at[k])

    once = (
        (outw_ref, outw), (qkv_ref, qkv), (fc2_half_ref, half_fc2),
        (fc1_grad_ref.at[:, half_of(dp, fc1_grad_ref.shape[1])], half_fc1), (kept_ref, kept), (late_ref, late_pair),
    )

    def once_load(k):
        return pltpu.make_async_copy(once[k][0], once[k][1], once_sem.at[k])

    grads = (fc2_grad_ref, fc1_grad_ref, outw_grad, qkv_grad)
    halves = (half_fc2, half_fc1, half_outw, half_qkv)
    dp_ins = (dp_fc2, dp_fc1, dp_outw, dp_qkv)
    row_ins = (row_fc2, row_fc1, row_outw, row_qkv)
    tots = (tot_fc2, tot_fc1, tot_outw, tot_qkv)

    codes = sorted(range(1, row_count), key=lambda code: (code & -code, -code)) + [0]

    def rows_at(code):
        return row_place(crossed(row, code), row_count, place, block)

    def dp_copy(w, code):
        full = grads[w]
        return copy_to(
            part_at(full, rows_at(code), other_half_of(dp, full.shape[-1])),
            part_at(dp_ins[w], rows_at(code), slice(None)),
            dp_send.at[w, code],
            dp_recv.at[w, code],
            dp_at,
        )

    def row_copy(w, code):
        return copy_to(
            part_at(halves[w], rows_at(code), slice(None)),
            row_ins[w].at[code],
            row_send.at[w, code],
            row_recv.at[w, code],
            {"row": crossed(row, code & -code)},
        )

    def tot_copy(w):
        part = part_at(tots[w], slice(None), half_of(dp, tots[w].shape[-1]))
        return copy_to(part, part, tot_send.at[w], tot_recv.at[w], dp_at)

    def add_to(w, code, term):
        at = (slice(None), rows_at(code), slice(None)) if len(halves[w].shape) == 3 else (rows_at(code), slice(None))
        halves[w][at] = (halves[w][at].astype(F32) + term.astype(F32)).astype(BF16)

    def dp_sum(w, code):
        dp_copy(w, code).wait_recv()
        at = (slice(None), rows_at(code), slice(None)) if len(halves[w].shape) == 3 else (rows_at(code), slice(None))
        add_to(w, code, dp_ins[w][at])

    def row_take(w, code):
        row_copy(w, code).wait_recv()
        add_to(w, code - (code & -code), row_ins[w][code])

    def row_first(w):
        for code in codes[:-1]:
            if code % 2:
                row_copy(w, code).start()

    def row_next(w):
        for code in codes[:-1]:
            if code % 2 == 0:
                far = 1
                while far < code & -code:
                    row_take(w, code + far)
                    far *= 2
                row_copy(w, code).start()

    def row_last(w):
        far = 1
        while far < row_count:
            row_take(w, far)
            far *= 2
        own = halves[w][:, rows_at(0), :] if len(halves[w].shape) == 3 else halves[w][rows_at(0), :]
        cols = half_of(dp, tots[w].shape[-1])
        if len(halves[w].shape) == 3:
            tots[w][:, :, cols] = own
        else:
            tots[w][:, cols] = own
        tot_copy(w).start()

    def given_copy(i):
        return copy_to(theirs.at[i], given.at[i], sum_send.at[0, i], sum_recv.at[0, i], core_at)

    def stat_copy(i):
        return copy_to(stat.at[i], stat_given.at[i], sum_send.at[1, i], sum_recv.at[1, i], core_at)

    def got_copy(i):
        return copy_to(send.at[i], got.at[i], sum_send.at[2, i], sum_recv.at[2, i], y_at)

    def stat_pair_copy(i):
        return copy_to(stat_pair.at[i], stat_in.at[i], sum_send.at[3, i], sum_recv.at[3, i], y_at)

    late_y = copy_to(late_ref, late_in, late_send.at[0], late_recv.at[0], y_at)
    late_core = copy_to(
        late_grad.at[:, pl.ds(0, 2 * local)], late_grad.at[:, pl.ds(2 * local, 2 * local)], late_send.at[1], late_recv.at[1], core_at
    )

    def move_copy(i):
        return copy_to(move_ref.at[i], move_in.at[i], move_send.at[i], move_recv.at[i], y_at)

    def small_copy(s):
        return copy_to(small.at[s], small_in.at[s], small_send.at[s], small_recv.at[s], rounds[s])

    late_y.start()
    for k in range(4):
        early_load(k, 0).start()
    once_load(2).start()
    once_load(0).start()
    for k in range(4):
        late_load(k, 0).start()
    for k in (1, 3, 5, 4):
        once_load(k).start()
    for i in range(count):
        move_copy(i).start()
    for code in codes:
        if code % 2 == 0:
            dp_copy(0, code).start()
    for code in codes:
        dp_copy(1, code).start()

    small[0] = jnp.zeros_like(small[0])
    small[0, 7:8, :] = mlp_bias_ref[1:2, :local]
    for part in range(mlp_bias_ref.shape[1] // local):
        small[0, 8 + part : 9 + part, :] = mlp_bias_ref[0:1, part * local : (part + 1) * local]
    qkv_sum[...] = jnp.zeros_like(qkv_sum)
    outw_sum[...] = jnp.zeros_like(outw_sum)
    once_load(2).wait()
    row_first(0)

    def product_of(span):
        terms = [
            lax.dot_general(mixed_grad[:, c * local : (c + 1) * local], qkv[c, span, :], NT, preferred_element_type=F32)
            for c in range(3)
        ]
        return terms[0] + terms[1] + terms[2]

    lane = lax.broadcasted_iota(jnp.int32, (1, two), 1)
    down = lax.broadcasted_iota(jnp.int32, (two, two), 0)
    across = lax.broadcasted_iota(jnp.int32, (two, two), 1)
    eye = (down == across).astype(BF16)

    @pl.loop(0, count)
    def _(i):
        for k in range(3):
            early_load(k, i).wait()

        @pl.when(i < count - 1)
        def _():
            early_load(3, i).wait()

        @pl.when(i == count - 1)
        def _():
            late_core.wait_recv()
            grad_in[...] = late_grad[...]

        values = source[i % 2].astype(F32) + total[...].astype(F32) + vectors_ref[4:5, :]
        middle = jnp.sum(values, axis=1, keepdims=True) / width
        square = jnp.sum(values * values, axis=1, keepdims=True) / width
        inverse = lax.rsqrt(square - middle * middle + NORM_EPS)
        normed = (values - middle) * inverse
        grad = grad_in[...].astype(F32)
        small[0, 5:6, :] += jnp.sum(grad[:, :local] * normed[:, :local], axis=0, keepdims=True)
        small[0, 6:7, :] += jnp.sum(grad[:, :local], axis=0, keepdims=True)
        scaled = grad * vectors_ref[2:3, :]
        first = jnp.sum(scaled, axis=1, keepdims=True) / width
        second = jnp.sum(scaled * normed, axis=1, keepdims=True) / width
        whole_grad = cot[...].astype(F32) + inverse * (scaled - first - normed * second)
        grad_hidden[i] = whole_grad[:, :local]
        small[0, 2:3, :] += jnp.sum(whole_grad[:, :local], axis=0, keepdims=True)
        hidden_low[...] = whole_grad.astype(BF16)

        @pl.when(i + 1 < count)
        def _():
            for k in range(3):
                early_load(k, i + 1).start()

        @pl.when(i + 2 < count)
        def _():
            early_load(3, i + 1).start()

        for k in range(4):
            late_load(k, i).wait()

        @pl.when(i == 0)
        def _():
            once_load(0).wait()
            once_load(1).wait()

        grad_att = jnp.dot(hidden_low[...], outw[...], preferred_element_type=F32).astype(BF16)
        for part in range(4):
            span = slice(part * local, (part + 1) * local)
            outw_sum[span, :] += lax.dot_general(hidden_low[:, span], att[...], TN, preferred_element_type=F32)
        for pair in range(local // two):
            base = pair * two
            cols = slice(pair * two, (pair + 1) * two)
            queries = mixed[:, cols]
            key_rows = mixed[:, local + base : local + base + two]
            value_rows = mixed[:, 2 * local + base : 2 * local + base + two]
            pair_grad = grad_att[:, cols]
            q_turned = lax.dot_general(eye, queries, NT, preferred_element_type=F32).astype(BF16)
            grad_turned = lax.dot_general(eye, pair_grad, NT, preferred_element_type=F32).astype(BF16)
            product = pair_grad.astype(F32) * att[:, cols].astype(F32)
            parts = []
            for side in range(2):
                mask = (lane // HEAD_DIM) == side
                turn = slice(side * HEAD_DIM, (side + 1) * HEAD_DIM)
                head_grad = jnp.where(mask, pair_grad, jnp.zeros_like(pair_grad))
                grad_probs = lax.dot_general(head_grad, value_rows, NT, preferred_element_type=F32)
                delta = jnp.sum(jnp.where(mask, product, 0.0), axis=1, keepdims=True)
                probs_low = probs[2 * pair + side]
                grad_scores = (probs_low.astype(F32) * (grad_probs - delta)).astype(BF16)
                parts.append(jnp.dot(grad_scores, key_rows, preferred_element_type=F32))
                k_turned[turn, :] = jnp.dot(q_turned[turn, :], grad_scores, preferred_element_type=F32)
                v_turned[turn, :] = jnp.dot(grad_turned[turn, :], probs_low, preferred_element_type=F32)
            q_grad = jnp.where((lane // HEAD_DIM) == 0, parts[0], parts[1]) * scale
            v_grad = v_turned[...].T
            mixed_grad[:, cols] = q_grad.astype(BF16)
            mixed_grad[:, local + base : local + base + two] = (k_turned[...].T * scale).astype(BF16)
            mixed_grad[:, 2 * local + base : 2 * local + base + two] = v_grad.astype(BF16)
            small[0, 0:1, cols] += jnp.sum(q_grad, axis=0, keepdims=True)
            small[0, 1:2, cols] += jnp.sum(v_grad, axis=0, keepdims=True)
        @pl.when(i + 1 < count)
        def _():
            for k in range(3):
                late_load(k, i + 1).start()

        values = source[i % 2].astype(F32)
        middle = jnp.sum(values, axis=1, keepdims=True) / width
        square = jnp.sum(values * values, axis=1, keepdims=True) / width
        inverse = lax.rsqrt(square - middle * middle + NORM_EPS)
        normed = (values - middle) * inverse
        normed1[i] = normed[:, :local]
        inverse1[i] = inverse
        scaled_in = normed * vectors_ref[0:1, :]
        far = product_of(slice(2 * local, 4 * local))
        theirs[i] = far.astype(BF16)
        given_copy(i).start()
        near = product_of(slice(0, 2 * local))
        mine[...] = near
        first = jnp.sum(far * vectors_ref[0:1, 2 * local :], axis=1, keepdims=True) + jnp.sum(
            near * vectors_ref[0:1, : 2 * local], axis=1, keepdims=True
        )
        second = jnp.sum(far * scaled_in[:, 2 * local :], axis=1, keepdims=True) + jnp.sum(
            near * scaled_in[:, : 2 * local], axis=1, keepdims=True
        )
        spread = jnp.where(lane == 0, first, jnp.where(lane == 1, second, 0.0))
        stat[i] = spread.T[:8, :]
        stat_copy(i).start()
        for part in range(4):
            span = slice(part * local, (part + 1) * local)
            term = lax.dot_general(low[:, span], mixed_grad[...], TN, preferred_element_type=F32)
            for c in range(3):
                qkv_sum[c, span, :] += term[:, c * local : (c + 1) * local]

        @pl.when(i + 1 < count)
        def _():
            late_load(3, i + 1).start()

        given_copy(i).wait_recv()
        kept_grad[i] = mine[:, :local] + given[i, :, :local].astype(F32)
        send[i] = (mine[:, local:] + given[i, :, local:].astype(F32)).astype(BF16)
        got_copy(i).start()
        stat_copy(i).wait_recv()
        stat_pair[i] = stat[i] + stat_given[i]
        stat_pair_copy(i).start()

        @pl.when(i == 0)
        def _():
            for code in codes:
                if code % 2 == 0:
                    dp_sum(0, code)
            row_next(0)
            once_load(3).wait()

        @pl.when(i == 1)
        def _():
            for code in codes:
                if code % 2:
                    dp_sum(1, code)
                    row_copy(1, code).start()

        @pl.when(i == count - 2)
        def _():
            once_load(5).wait()
            late_y.wait_recv()
            late_grad[:, :local] = (late_pair[:, :local].astype(F32) + late_in[:, local:].astype(F32)).astype(BF16)
            late_grad[:, local : 2 * local] = (late_pair[:, local:].astype(F32) + late_in[:, :local].astype(F32)).astype(BF16)
            late_core.start()

    outw_grad[...] = outw_sum[...].astype(BF16)
    half_outw[...] = outw_grad[:, half_of(dp, local)]
    for code in codes:
        dp_copy(2, code).start()
    qkv_grad[...] = qkv_sum[...].astype(BF16)
    half_qkv[...] = qkv_grad[:, :, half_of(dp, local)]
    for code in codes:
        dp_copy(3, code).start()
    for code in codes:
        if code % 2 == 0:
            dp_sum(1, code)
    row_next(1)
    row_last(0)
    once_load(4).wait()

    @pl.loop(0, count)
    def _(i):
        move_copy(i).wait_recv()
        finished[i] = (kept[i] + move_in[i].astype(F32)).astype(BF16)

    for w in (2, 3):
        for code in codes:
            if code % 2:
                dp_sum(w, code)
                row_copy(w, code).start()
    row_last(1)

    for w in (2, 3):
        for code in codes:
            if code % 2 == 0:
                dp_sum(w, code)
        row_next(w)

    @pl.loop(0, count)
    def _(i):
        got_copy(i).wait_recv()
        stat_pair_copy(i).wait_recv()
        sums = stat_pair[i] + stat_in[i]
        spread = jnp.concatenate([sums, jnp.zeros((two - 8, rows), F32)], axis=0).T / width
        grad = kept_grad[i] + got[i].astype(F32)
        small[0, 3:4, :] += jnp.sum(grad * normed1[i], axis=0, keepdims=True)
        small[0, 4:5, :] += jnp.sum(grad, axis=0, keepdims=True)
        scaled = grad * vectors_ref[0:1, :local]
        grad_hidden[i] += inverse1[i] * (scaled - spread[:, 0:1] - normed1[i] * spread[:, 1:2])

    pltpu.make_async_copy(finished, images_out, out_sem.at[0]).start()
    pltpu.make_async_copy(grad_hidden, images_grad_out, out_sem.at[1]).start()
    small_copy(0).start()
    row_last(2)
    row_last(3)
    for s in range(len(rounds)):
        small_copy(s).wait_recv()
        small[s + 1] = small[s] + small_in[s]
        if s + 1 < len(rounds):
            small_copy(s + 1).start()
    outs = ((tot_fc2, fc2_out), (tot_fc1, fc1_out), (tot_outw, outw_out), (tot_qkv, qkv_out))
    for w, (here, there) in enumerate(outs):
        tot_copy(w).wait_recv()
        pltpu.make_async_copy(here, there, out_sem.at[2 + w]).start()
    small_out[...] = small[len(rounds)]
    for i in range(count):
        given_copy(i).wait_send()
        stat_copy(i).wait_send()
        got_copy(i).wait_send()
        stat_pair_copy(i).wait_send()
        move_copy(i).wait_send()
    late_y.wait_send()
    late_core.wait_send()
    for s in range(len(rounds)):
        small_copy(s).wait_send()
    for w in range(4):
        tot_copy(w).wait_send()
        for code in codes:
            if w or code % 2 == 0:
                dp_copy(w, code).wait_send()
            if code:
                row_copy(w, code).wait_send()
    for k, (here, there) in enumerate(((finished, images_out), (grad_hidden, images_grad_out), *outs)):
        pltpu.make_async_copy(here, there, out_sem.at[k]).wait()


def back(
    source, total, cot, grad_low, mixed, probs, att, low, move, kept, qkv, outw, fc1_grad, fc2_half, fc2_grad, late, vectors, mlp_bias
):
    count, rows, width = source.shape
    local = width // 4
    row_count = lax.axis_size("row")
    block = width // row_count
    hidden = fc1_grad.shape[1]
    qkv_width = 3 * local
    heads = local // HEAD_DIM
    rounds = row_count.bit_length()
    outs = [
        ((count, rows, local), BF16), ((count, rows, local), F32), ((16, local), F32),
        ((3, block, local), BF16), ((block, local), BF16), ((block, hidden), BF16), ((block, hidden), BF16),
    ]
    own_f32 = ((count, rows, local), F32)
    own_low = ((count, rows, local), BF16)
    pair_low = ((count, rows, 2 * local), BF16)
    stat = ((count, 8, rows), F32)
    wide = ((rows, width), BF16)
    turned = ((2 * HEAD_DIM, rows), F32)
    columns = (((), hidden), ((), hidden), ((), local), ((3,), local))
    scratch = [
        ((2, rows, width), BF16), wide, wide, wide, ((rows, qkv_width), BF16), ((heads, rows, rows), BF16), ((rows, local), BF16), wide,
        wide, ((rows, qkv_width), BF16), own_f32, own_f32, ((count, rows, 1), F32),
        ((3, width, local), F32), ((width, local), F32), turned, turned,
        pair_low, pair_low, ((rows, 2 * local), F32), own_f32, own_low, own_low, stat, stat, stat, stat,
        ((rows, 2 * local), BF16), ((rows, 2 * local), BF16), wide, own_low, own_f32, own_low, ((3, width, local), BF16), ((width, local), BF16),
        ((3, width, local), BF16), ((width, local), BF16), ((rounds + 1, 16, local), F32), ((rounds, 16, local), F32),
        *[((*lead, width, c // 2), BF16) for lead, c in columns],
        *[((*lead, width, c // 2), BF16) for lead, c in columns],
        *[((row_count, *lead, block, c // 2), BF16) for lead, c in columns],
        *[((*lead, block, c), BF16) for lead, c in columns],
    ]
    dma = pltpu.SemaphoreType.DMA
    whole = pl.BlockSpec(memory_space=pl.ANY)
    vmem = pl.BlockSpec(memory_space=pltpu.VMEM)
    return pl.pallas_call(
        functools.partial(back_kernel, (count, rows, local, row_count)),
        out_shape=[jax.ShapeDtypeStruct(*s) for s in outs],
        in_specs=[whole] * 16 + [vmem] * 2,
        out_specs=[whole, whole, vmem] + [whole] * 4,
        scratch_shapes=[pltpu.VMEM(*s) for s in scratch]
        + [dma((4,)), dma((4,)), dma((6,)), dma((4, count)), dma((4, count)), dma((count,)), dma((count,)), dma((rounds,)), dma((rounds,))]
        + [dma((4, row_count))] * 4
        + [dma((4,)), dma((4,)), dma((2,)), dma((2,)), dma((6,))],
        name="back",
        compiler_params=pltpu.CompilerParams(
            vmem_limit_bytes=63 * 2**20, collective_id=2, has_side_effects=True
        ),
    )(source, total, cot, grad_low, mixed, probs, att, low, move, kept, qkv, outw, fc1_grad, fc2_half, fc2_grad, late, vectors, mlp_bias)


def adam_step(weight, grad, momentum, variance):
    moment_new = BETA_FIRST * momentum + (1.0 - BETA_FIRST) * grad
    second_new = BETA_SECOND * variance + (1.0 - BETA_SECOND) * grad * grad
    corrected = moment_new / (1.0 - BETA_FIRST**STEP)
    second_corrected = second_new / (1.0 - BETA_SECOND**STEP)
    master = weight.astype(jnp.float32)
    updated = master - LEARN_RATE * (
        corrected / (jnp.sqrt(second_corrected) + ADAM_EPS) + WEIGHT_DECAY * master
    )
    return (updated, moment_new, second_new)


def per_device(
    images_in,
    cotangent,
    first_gain,
    first_shift,
    second_gain,
    second_shift,
    qkv_weight,
    qv_bias,
    out_weight,
    out_bias,
    fc1_weight,
    fc1_bias,
    fc2_weight,
    fc2_bias,
    qkv_momentum,
    qkv_variance,
    out_momentum,
    out_variance,
    fc1_momentum,
    fc1_variance,
    fc2_momentum,
    fc2_variance,
):
    image_count, seq, local = images_in.shape
    width = 4 * local
    rows = -(-seq // ROW_TILE) * ROW_TILE
    place = lax.axis_index("col")

    vectors = [v[None] for v in (first_gain, first_shift, second_gain, second_shift, out_bias)]
    (
        source_all, cot_all, low_all, mixed_all, probs_all, att_all, total_all, grad_low2, qkv_full, out_full, vectors,
        move, kept, fc1_grad, fc2_half, fc2_grad, late, mlp_bias,
    ) = ahead(
        jnp.pad(images_in, ((0, 0), (0, rows - seq), (0, 0))),
        jnp.pad(cotangent, ((0, 0), (0, rows - seq), (0, 0))),
        qkv_weight.transpose(1, 0, 2),
        out_weight,
        fc1_weight,
        fc2_weight,
        vectors,
        qv_bias,
        fc1_bias[None],
        fc2_bias[None],
        seq,
    )
    images_out, images_grad, small, qkv_total, out_total, fc1_total, fc2_total = back(
        source_all, total_all, cot_all, grad_low2, mixed_all, probs_all, att_all, low_all, move, kept,
        qkv_full, out_full, fc1_grad, fc2_half, fc2_grad, late, vectors, mlp_bias,
    )
    qkv_total = qkv_total.transpose(1, 0, 2).astype(F32)
    out_total, fc1_total, fc2_total = (t.astype(F32) for t in (out_total, fc1_total, fc2_total))
    qkv_new = adam_step(qkv_weight, qkv_total, qkv_momentum, qkv_variance)
    out_new = adam_step(out_weight, out_total, out_momentum, out_variance)
    fc1_new = adam_step(fc1_weight, fc1_total, fc1_momentum, fc1_variance)
    fc2_new = adam_step(fc2_weight, fc2_total, fc2_momentum, fc2_variance)
    return (
        images_out[:, :seq],
        images_grad[:, :seq],
        qkv_total,
        out_total,
        fc1_total,
        fc2_total,
        small[0:2],
        small[2],
        small[8:12].reshape(-1),
        small[7],
        small[3],
        small[4],
        small[5],
        small[6],
        qkv_new[0],
        out_new[0],
        fc1_new[0],
        fc2_new[0],
        qkv_new[1],
        out_new[1],
        fc1_new[1],
        fc2_new[1],
        qkv_new[2],
        out_new[2],
        fc1_new[2],
        fc2_new[2],
    )


def solution(mesh):
    return jax.shard_map(
        per_device,
        mesh=mesh,
        in_specs=(
            P(("dp", "row"), None, "col"),
            P(("dp", "row"), None, "col"),
            P("col"),
            P("col"),
            P("col"),
            P("col"),
            P("row", None, "col"),
            P(None, "col"),
            P("row", "col"),
            P("col"),
            P("row", "col"),
            P("col"),
            P("row", "col"),
            P("col"),
            P("row", None, "col"),
            P("row", None, "col"),
            P("row", "col"),
            P("row", "col"),
            P("row", "col"),
            P("row", "col"),
            P("row", "col"),
            P("row", "col"),
        ),
        out_specs=(
            P(("dp", "row"), None, "col"),
            P(("dp", "row"), None, "col"),
            P("row", None, "col"),
            P("row", "col"),
            P("row", "col"),
            P("row", "col"),
            P(None, "col"),
            P("col"),
            P("col"),
            P("col"),
            P("col"),
            P("col"),
            P("col"),
            P("col"),
            P("row", None, "col"),
            P("row", "col"),
            P("row", "col"),
            P("row", "col"),
            P("row", None, "col"),
            P("row", "col"),
            P("row", "col"),
            P("row", "col"),
            P("row", None, "col"),
            P("row", "col"),
            P("row", "col"),
            P("row", "col"),
        ),
        check_vma=False,
    )
```

profile of v0, /device:TPU:0, one launch (start us, length us, event | category | flops | bytes accessed | tf_op | source)
XLA Modules:
  0.0 234.2 jit_solution(1040532644929050694)
XLA Ops:
  0.7 0.0 copy-start.8
  0.7 2.2 pad.7.images_ref
  2.9 0.0 copy-done.8
  2.9 1.0 pad.8.cot_ref
  3.9 129.4 %ahead.1 = (bf16[3,592,1024]{2,1,0:T(8,128)(2,1)}, bf16[3,592,1024]{2,1,0:T(8,128)(2,1)}, bf16[3,592,1024]{2,1,0:T(8,128)(2,1)}, bf16[3,592,768]{2,1,0:T(8,128)(...) custom-call(bf16[3,592,256]{2,1,0:T(8,128)(2,1)} %pad.7.images_ref, ...), custom_call_target="tpu_custom_call" | custom-call | tf_op jit(solution)/shard_map/ahead/pallas_call | solution.py:512
  133.4 0.0 copy-start.13
  133.4 0.0 copy-start.15
  133.4 0.0 copy-start.16
  133.4 83.2 %back.1 = (bf16[3,592,256]{2,1,0:T(8,128)(2,1)}, f32[3,592,256]{2,1,0:T(8,128)}, f32[16,256]{1,0:T(8,128)}, bf16[3,256,256]{2,1,0:T(8,128)(2,1)}, bf16[256,256]{...) custom-call(bf16[3,592,1024]{2,1,0:T(8,128)(2,1)} %get-tuple-element.51.source_ref, ...), custom_call_target="tpu_custom_call" | custom-call | tf_op jit(solution)/shard_map/back/pallas_call | solution.py:979
  216.6 0.0 copy-start.2
  216.6 2.3 slice.30
  218.9 1.3 slice.32
  220.2 0.7 slice_bitcast_fusion
  220.9 1.5 fusion.16
  222.4 0.6 copy.48
  223.0 0.0 copy-done.13
  223.0 0.0 copy-done.15
  223.0 0.0 copy-done.16
  223.0 0.0 copy-start.3
  223.0 0.0 copy-start.9
  223.0 0.0 copy-start.10
  223.0 0.0 copy-start.14
  223.0 2.1 convert_subtract_fusion.3
  225.1 0.0 copy-done.2
  225.1 0.0 copy-start.11
  225.1 0.0 copy-start.12
  225.1 1.3 slice.31
  226.5 0.0 copy-done.3
  226.5 0.0 copy-done.9
  226.5 0.0 copy-done.10
  226.5 0.0 copy-done.14
  226.5 0.0 copy-start
  226.5 0.0 copy-start.1
  226.5 0.0 copy-start.4
  226.5 0.0 copy-start.5
  226.5 0.0 copy-start.6
  226.5 0.0 copy-start.7
  226.5 1.9 convert_subtract_fusion.2
  228.4 0.0 copy-done.11
  228.4 0.0 copy-done.12
  228.4 0.0 copy-done
  228.4 0.0 copy-done.1
  228.4 0.5 copy-done.4
  228.9 0.6 copy-done.5
  229.5 0.3 copy-done.6
  229.8 0.3 copy-done.7
  230.1 4.0 %convert_subtract_fusion = (f32[256,1024]{1,0:T(8,128)}, f32[256,1024]{1,0:T(8,128)}, f32[256,1024]{1,0:T(8,128)}, f32[256,1024]{1,0:T(8,128)}, f32[256,1024]{1,...) fusion(bf16[256,1024]{1,0:T(8,128)(2,1)S(1)} %copy-done.1, ...), kind=kLoop, calls=%fused_computation.2 | loop fusion | flops 8912896 | bytes 14680064 | tf_op jit(solution)/shard_map/sub | solution.py:1001
Async XLA Ops:
  0.7 2.2 copy-start.8
  133.4 89.6 %copy-start.13 = (bf16[256,256]{1,0:T(8,128)(2,1)S(1)}, bf16[256,256]{1,0:T(8,128)(2,1)}, u32[]{:S(2)}) copy-start(bf16[256,256]{1,0:T(8,128)(2,1)} %out_ref.1) | copy-start | bytes 393220
  133.4 89.6 %copy-start.15 = (f32[256,256]{1,0:T(8,128)S(1)}, f32[256,256]{1,0:T(8,128)}, u32[]{:S(2)}) copy-start(f32[256,256]{1,0:T(8,128)} %param.38) | copy-start | bytes 786436
  133.4 89.6 %copy-start.16 = (f32[256,256]{1,0:T(8,128)S(1)}, f32[256,256]{1,0:T(8,128)}, u32[]{:S(2)}) copy-start(f32[256,256]{1,0:T(8,128)} %param.39) | copy-start | bytes 786436
  216.6 8.5 %copy-start.2 = (f32[3,592,256]{2,1,0:T(8,128)S(1)}, f32[3,592,256]{2,1,0:T(8,128)}, u32[]{:S(2)}) copy-start(f32[3,592,256]{2,1,0:T(8,128)} %get-tuple-element.70) | copy-start | bytes 5455876
  223.0 3.5 %copy-start.3 = (bf16[256,3,256]{2,0,1:T(8,128)(2,1)S(1)}, bf16[256,3,256]{2,0,1:T(8,128)(2,1)}, u32[]{:S(2)}) copy-start(bf16[256,3,256]{2,0,1:T(8,128)(2,1)} %param.28) | copy-start | bytes 1179652
  223.0 3.5 %copy-start.9 = (f32[256,3,256]{2,0,1:T(8,128)S(1)}, f32[256,3,256]{2,0,1:T(8,128)}, u32[]{:S(2)}) copy-start(f32[256,3,256]{2,0,1:T(8,128)} %param.36) | copy-start | bytes 2359300
  223.0 3.4 %copy-start.10 = (f32[256,3,256]{2,0,1:T(8,128)S(1)}, f32[256,3,256]{2,0,1:T(8,128)}, u32[]{:S(2)}) copy-start(f32[256,3,256]{2,0,1:T(8,128)} %param.37) | copy-start | bytes 2359300
  223.0 3.4 %copy-start.14 = (bf16[3,256,256]{2,1,0:T(8,128)(2,1)S(1)}, bf16[3,256,256]{2,1,0:T(8,128)(2,1)}, u32[]{:S(2)}) copy-start(bf16[3,256,256]{2,1,0:T(8,128)(2,1)} %get-tuple-element.71) | copy-start | bytes 1179652
  225.1 3.3 %copy-start.11 = (bf16[256,1024]{1,0:T(8,128)(2,1)S(1)}, bf16[256,1024]{1,0:T(8,128)(2,1)}, u32[]{:S(2)}) copy-start(bf16[256,1024]{1,0:T(8,128)(2,1)} %get-tuple-element.73) | copy-start | bytes 1572868
  225.1 3.3 %copy-start.12 = (bf16[256,1024]{1,0:T(8,128)(2,1)S(1)}, bf16[256,1024]{1,0:T(8,128)(2,1)}, u32[]{:S(2)}) copy-start(bf16[256,1024]{1,0:T(8,128)(2,1)} %get-tuple-element.74) | copy-start | bytes 1572868
  226.5 2.0 copy-start
  226.5 1.9 copy-start.1
  226.5 2.5 %copy-start.4 = (f32[256,1024]{1,0:T(8,128)S(1)}, f32[256,1024]{1,0:T(8,128)}, u32[]{:S(2)}) copy-start(f32[256,1024]{1,0:T(8,128)} %param.42) | copy-start | bytes 3145732
  226.5 3.0 %copy-start.5 = (f32[256,1024]{1,0:T(8,128)S(1)}, f32[256,1024]{1,0:T(8,128)}, u32[]{:S(2)}) copy-start(f32[256,1024]{1,0:T(8,128)} %param.43) | copy-start | bytes 3145732
  226.5 3.3 %copy-start.6 = (f32[256,1024]{1,0:T(8,128)S(1)}, f32[256,1024]{1,0:T(8,128)}, u32[]{:S(2)}) copy-start(f32[256,1024]{1,0:T(8,128)} %param.41) | copy-start | bytes 3145732
  226.5 3.6 %copy-start.7 = (f32[256,1024]{1,0:T(8,128)S(1)}, f32[256,1024]{1,0:T(8,128)}, u32[]{:S(2)}) copy-start(f32[256,1024]{1,0:T(8,128)} %param.40) | copy-start | bytes 3145732
where the time goes:
time: 235 us; the launch traced here: 234 us
  Pallas kernels  213 us (91%)
  local copies, waits for them, and re-layouts  12.7 us (5%)
  other arithmetic  7.97 us (3%)
    pallas_call x1, Pallas kernels, ahead(): pl.pallas_call(functools.partial(ahead_kernel, (count, seq, rows, local,...  129 us
    pallas_call x1, Pallas kernels, back(): pl.pallas_call(functools.partial(back_kernel, (count, rows, local, row_co...  83.2 us
    sub x3, other arithmetic, adam_step(): master - LEARN_RATE * (corrected / (jnp.sqrt(second_corrected) + ADAM_EPS...  7.97 us

commit v1 on v0

--- a/solution.py
+++ b/solution.py
@@ -1004,6 +1004,67 @@
     return (updated, moment_new, second_new)
 
 
+def update_kernel(seq, *refs):
+    images_in, grad_in, small = refs[:3]
+    blocks = refs[3:19]
+    images_out, grad_out = refs[19:21]
+    grads = refs[21:25]
+    sums = refs[25:33]
+    fresh = refs[33:45]
+    images_out[...] = images_in[:, :seq, :]
+    grad_out[...] = grad_in[:, :seq, :]
+    sums[0][...] = small[0:2, :]
+    local = small.shape[1]
+    for k, line in enumerate((2, None, 7, 3, 4, 5, 6)):
+        if line is None:
+            for part in range(4):
+                sums[k + 1][:, part * local : (part + 1) * local] = small[8 + part : 9 + part, :]
+        else:
+            sums[k + 1][...] = small[line : line + 1, :]
+    for w in range(4):
+        weight, total, momentum, variance = (blocks[4 * w + k] for k in range(4))
+        grad = total[...].astype(F32)
+        grads[w][...] = grad
+        updated, moment_new, second_new = adam_step(weight[...], grad, momentum[...], variance[...])
+        fresh[w][...] = updated
+        fresh[4 + w][...] = moment_new
+        fresh[8 + w][...] = second_new
+
+
+def update(images, images_grad, small, blocks, seq):
+    count, rows, local = images.shape
+    steps = 4
+
+    def image_spec(lines):
+        return pl.BlockSpec((1, lines, local), lambda i: (jnp.minimum(i, count - 1), 0, 0))
+
+    def rows_spec(shape):
+        if len(shape) == 3:
+            return pl.BlockSpec((shape[0], shape[1] // steps, shape[2]), lambda i: (0, i, 0))
+        return pl.BlockSpec((shape[0] // steps, shape[1]), lambda i: (i, 0))
+
+    def whole_spec(shape):
+        return pl.BlockSpec(shape, lambda i: (0, 0))
+
+    flat = [array for group in blocks for array in group]
+    shapes = [group[0].shape for group in blocks]
+    hidden = shapes[2][1]
+    sum_shapes = [(2, local), (1, local), (1, hidden), *[(1, local)] * 5]
+    outs = [((count, seq, local), BF16), ((count, seq, local), F32)]
+    outs += [(shape, F32) for shape in (*shapes, *sum_shapes, *shapes, *shapes, *shapes)]
+    out_specs = [image_spec(seq), image_spec(seq), *[rows_spec(s) for s in shapes], *[whole_spec(s) for s in sum_shapes]]
+    out_specs += [rows_spec(s) for s in shapes] * 3
+    return pl.pallas_call(
+        functools.partial(update_kernel, seq),
+        grid=(steps,),
+        out_shape=[jax.ShapeDtypeStruct(*s) for s in outs],
+        in_specs=[image_spec(rows), image_spec(rows), whole_spec(small.shape), *[rows_spec(a.shape) for a in flat]],
+        out_specs=out_specs,
+        name="update",
+        compiler_params=pltpu.CompilerParams(vmem_limit_bytes=63 * 2**20),
+    )(images, images_grad, small, *flat)
+
+
 def per_device(
     images_in,
     cotangent,
@@ -1054,40 +1115,23 @@
         source_all, total_all, cot_all, grad_low2, mixed_all, probs_all, att_all, low_all, move, kept,
         qkv_full, out_full, fc1_grad, fc2_half, fc2_grad, late, vectors, mlp_bias,
     )
-    qkv_total = qkv_total.transpose(1, 0, 2).astype(F32)
-    out_total, fc1_total, fc2_total = (t.astype(F32) for t in (out_total, fc1_total, fc2_total))
-    qkv_new = adam_step(qkv_weight, qkv_total, qkv_momentum, qkv_variance)
-    out_new = adam_step(out_weight, out_total, out_momentum, out_variance)
-    fc1_new = adam_step(fc1_weight, fc1_total, fc1_momentum, fc1_variance)
-    fc2_new = adam_step(fc2_weight, fc2_total, fc2_momentum, fc2_variance)
-    return (
-        images_out[:, :seq],
-        images_grad[:, :seq],
-        qkv_total,
-        out_total,
-        fc1_total,
-        fc2_total,
-        small[0:2],
-        small[2],
-        small[8:12].reshape(-1),
-        small[7],
-        small[3],
-        small[4],
-        small[5],
-        small[6],
-        qkv_new[0],
-        out_new[0],
-        fc1_new[0],
-        fc2_new[0],
-        qkv_new[1],
-        out_new[1],
-        fc1_new[1],
-        fc2_new[1],
-        qkv_new[2],
-        out_new[2],
-        fc1_new[2],
-        fc2_new[2],
+    def turned(value):
+        return value.transpose(1, 0, 2)
+
+    results = update(
+        images_out,
+        images_grad,
+        small,
+        (
+            (turned(qkv_weight), qkv_total, turned(qkv_momentum), turned(qkv_variance)),
+            (out_weight, out_total, out_momentum, out_variance),
+            (fc1_weight, fc1_total, fc1_momentum, fc1_variance),
+            (fc2_weight, fc2_total, fc2_momentum, fc2_variance),
+        ),
+        seq,
     )
+    results = [turned(r) if k in (2, 14, 18, 22) else r for k, r in enumerate(results)]
+    return tuple(r.reshape(-1) if 7 <= k < 14 else r for k, r in enumerate(results))
 
 
 def solution(mesh):

time: 235 us -> 228 us (0.970)
  Pallas kernels: 213 us -> 224 us
  local copies, waits for them, and re-layouts: 12.7 us -> 3.22 us
  other arithmetic: 7.97 us -> 0 us
    pallas_call x0 -> x1, Pallas kernels: none -> 11.1 us  [update(): pl.pallas_call(functools.partial(update_kernel, seq), grid=(steps,), out_...]
    sub x3 -> x0, other arithmetic: 7.97 us -> none  [adam_step(): master - LEARN_RATE * (corrected / (jnp.sqrt(second_corrected) + ADAM_EPS...]
    slice x4 -> x0, local copies, waits for them, and re-layouts: 6.39 us -> none  [the longest x1 2.28 us: per_device(): images_out[:, :seq]]
    unnamed x36 -> x2, local copies, waits for them, and re-layouts: 3.08 us -> 0.01 us
where the time goes in v1:
time: 228 us
  Pallas kernels  224 us (98%)
  local copies, waits for them, and re-layouts  3.22 us (1%)
    pallas_call x1, Pallas kernels, ahead(): pl.pallas_call(functools.partial(ahead_kernel, (count, seq, rows, local,...  129 us
    pallas_call x1, Pallas kernels, back(): pl.pallas_call(functools.partial(back_kernel, (count, rows, local, row_co...  83.2 us
    pallas_call x1, Pallas kernels, update(): pl.pallas_call(functools.partial(update_kernel, seq), grid=(steps,), out_...  11.1 us

profile of v1, /device:TPU:0, one launch (start us, length us, event | category | flops | bytes accessed | tf_op | source)
XLA Modules:
  0.0 227.9 jit_solution(3716278274545298613)
XLA Ops:
  0.7 0.0 copy-start
  0.7 2.2 pad.7.images_ref
  2.9 0.0 copy-done
  2.9 1.0 pad.8.cot_ref
  3.9 129.5 %ahead.1 = (bf16[3,592,1024]{2,1,0:T(8,128)(2,1)}, bf16[3,592,1024]{2,1,0:T(8,128)(2,1)}, bf16[3,592,1024]{2,1,0:T(8,128)(2,1)}, bf16[3,592,768]{2,1,0:T(8,128)(...) custom-call(bf16[3,592,256]{2,1,0:T(8,128)(2,1)} %pad.7.images_ref, ...), custom_call_target="tpu_custom_call" | custom-call | tf_op jit(solution)/shard_map/ahead/pallas_call | solution.py:512
  133.4 83.2 %back.1 = (bf16[3,592,256]{2,1,0:T(8,128)(2,1)}, f32[3,592,256]{2,1,0:T(8,128)}, f32[16,256]{1,0:T(8,128)}, bf16[3,256,256]{2,1,0:T(8,128)(2,1)}, bf16[256,256]{...) custom-call(bf16[3,592,1024]{2,1,0:T(8,128)(2,1)} %get-tuple-element.77.source_ref, ...), custom_call_target="tpu_custom_call" | custom-call | tf_op jit(solution)/shard_map/back/pallas_call | solution.py:979
  216.6 11.1 %update.1 = (bf16[3,577,256]{2,1,0:T(8,128)(2,1)}, f32[3,577,256]{2,1,0:T(8,128)}, f32[3,256,256]{2,1,0:T(8,128)}, f32[256,256]{1,0:T(8,128)}, f32[256,1024]{1,0...) custom-call(bf16[3,592,256]{2,1,0:T(8,128)(2,1)} %get-tuple-element., ...), custom_call_target="tpu_custom_call" | custom-call | tf_op jit(solution)/shard_map/update/pallas_call | solution.py:1057
Async XLA Ops:
  0.7 2.2 copy-start

commit v2 on v1

--- a/solution.py
+++ b/solution.py
@@ -330,8 +330,6 @@
             for code in codes[:2]:
                 relay(3, code)
 
-    for code in codes[2:]:
-        relay(3, code)
     outs = ((qkv_full, qkv_out), (out_full, outw_out), (vectors, vectors_out), (cot, cot_out), (move, move_out), (kept, kept_out), (fc1_grad, fc1_grad_out), (fc2_half, fc2_half_out), (fc2_grad, fc2_grad_out), (total.at[pl.ds(0, count - 1)], grad_out))
 
     def out_copy(k):
@@ -342,8 +340,6 @@
     bias_out[...] = jnp.zeros_like(bias_out)
     step = hidden_width // 4
     given_copy(count - 1).wait_send()
-    arrived(2)
-    arrived(3)
 
     @pl.loop(0, count)
     def _(i):
@@ -353,6 +349,12 @@
         total[i, :, :local] = (pair[i, :, :local].astype(F32) + pair_in[i, :, local:].astype(F32)).astype(BF16)
         total[i, :, local : 2 * local] = (pair[i, :, local:].astype(F32) + pair_in[i, :, :local].astype(F32)).astype(BF16)
         total_copy(i).start()
+
+        @pl.when(i == 0)
+        def _():
+            for code in codes[2:]:
+                relay(3, code)
+
         image_copy(1, i).wait()
         pair_copy(i).wait_send()
         here_copy(1, i).wait()
@@ -367,6 +369,12 @@
         square = jnp.sum(values * values, axis=1, keepdims=True) / width
         inverse = lax.rsqrt(square - middle * middle + NORM_EPS)
         low[i] = ((values - middle) * inverse * vectors[2:3, :] + vectors[3:4, :]).astype(BF16)
+
+        @pl.when(i == 0)
+        def _():
+            arrived(2)
+            arrived(3)
+
         @pl.loop(0, 4)
         def _(part):
             cols = pl.ds(pl.multiple_of(part * step, step), step)

time: 228 us -> 225 us (0.987)
  Pallas kernels: 224 us -> 221 us
    pallas_call x1, Pallas kernels: 129 us -> 126 us  [ahead(): pl.pallas_call(functools.partial(ahead_kernel, (count, seq, rows, local,...]
where the time goes in v2:
time: 225 us
  Pallas kernels  221 us (98%)
  local copies, waits for them, and re-layouts  3.22 us (1%)
    pallas_call x1, Pallas kernels, ahead(): pl.pallas_call(functools.partial(ahead_kernel, (count, seq, rows, local,...  126 us
    pallas_call x1, Pallas kernels, back(): pl.pallas_call(functools.partial(back_kernel, (count, rows, local, row_co...  83.6 us
    pallas_call x1, Pallas kernels, update(): pl.pallas_call(functools.partial(update_kernel, seq), grid=(steps,), out_...  11.1 us

profile of v2, /device:TPU:0, one launch (start us, length us, event | category | flops | bytes accessed | tf_op | source)
XLA Modules:
  0.0 224.8 jit_solution(1607644703916405911)
XLA Ops:
  0.7 0.0 copy-start
  0.7 2.2 pad.7.images_ref
  2.9 0.0 copy-done
  2.9 1.0 pad.8.cot_ref
  3.9 126.0 %ahead.1 = (bf16[3,592,1024]{2,1,0:T(8,128)(2,1)}, bf16[3,592,1024]{2,1,0:T(8,128)(2,1)}, bf16[3,592,1024]{2,1,0:T(8,128)(2,1)}, bf16[3,592,768]{2,1,0:T(8,128)(...) custom-call(bf16[3,592,256]{2,1,0:T(8,128)(2,1)} %pad.7.images_ref, ...), custom_call_target="tpu_custom_call" | custom-call | tf_op jit(solution)/shard_map/ahead/pallas_call | solution.py:520
  129.9 83.6 %back.1 = (bf16[3,592,256]{2,1,0:T(8,128)(2,1)}, f32[3,592,256]{2,1,0:T(8,128)}, f32[16,256]{1,0:T(8,128)}, bf16[3,256,256]{2,1,0:T(8,128)(2,1)}, bf16[256,256]{...) custom-call(bf16[3,592,1024]{2,1,0:T(8,128)(2,1)} %get-tuple-element.77.source_ref, ...), custom_call_target="tpu_custom_call" | custom-call | tf_op jit(solution)/shard_map/back/pallas_call | solution.py:987
  213.5 11.1 %update.1 = (bf16[3,577,256]{2,1,0:T(8,128)(2,1)}, f32[3,577,256]{2,1,0:T(8,128)}, f32[3,256,256]{2,1,0:T(8,128)}, f32[256,256]{1,0:T(8,128)}, f32[256,1024]{1,0...) custom-call(bf16[3,592,256]{2,1,0:T(8,128)(2,1)} %get-tuple-element., ...), custom_call_target="tpu_custom_call" | custom-call | tf_op jit(solution)/shard_map/update/pallas_call | solution.py:1065
Async XLA Ops:
  0.7 2.2 %copy-start = (bf16[3,577,256]{2,1,0:T(8,128)(2,1)S(1)}, bf16[3,577,256]{2,1,0:T(8,128)(2,1)}, u32[]{:S(2)}) copy-start(bf16[3,577,256]{2,1,0:T(8,128)(2,1)} %param.23) | copy-start | bytes 2658820
